TPU v7x, 32 devices: a whole 2x2x4 slice. The times are simulated.
32 devices in a mesh: ops: 8 (over z, core), blk: 4 (over y, x).
Axes of the slice: x: 2, y: 2, z: 4, core: 2. Of those that a mesh axis runs over, the one named last changes fastest.
Arguments:
- psi: bfloat16 [2048, 1024], P('blk'), may hold values from -6 to 6
- left_blocks: bfloat16 [64, 16, 128, 128], P('ops', 'blk'), may hold values from -0.5 to 0.5
- right_ops: bfloat16 [64, 1024, 1024], P(('ops', 'blk')), may hold values from -0.046875 to 0.046875
- block_target: int32 [64, 16], P('ops'), may hold values from 0 to 15
- left_partner: int32 [64], P('ops'), may hold values from 0 to 63, as said below
- block_len: int32 [16], replicated, may hold values from 1 to 128, 1536 in all
Outputs:
- sigma: bfloat16 [2048, 1024], P('blk', 'ops')
Inputs may be any that keep to these rules, and one draw needn't show every extreme that they name: left_partner is a permutation of 0 to 63 that maps each aligned group of 8 operators onto itself.
All inputs are finite; a program needn't handle non-finite values.
Results may differ from a plain program's by a relative error of at most 0.018.
Values may be sent and summed in bfloat16 or wider, within the bound.
A program may use at most 128 MiB of HBM per device.

v0:
```python
import functools

import jax
import jax.numpy as jnp
from jax import lax
from jax.experimental import pallas as pl
from jax.experimental.pallas import tpu as pltpu
from jax.sharding import PartitionSpec as P

MESH = pl.DeviceIdType.MESH
VMEM = pltpu.VMEM
DMA = pltpu.SemaphoreType.DMA


def across(c, d, n):
    out, bit = 0, 1
    while bit < n:
        have = (c // bit) % 2
        out = out + bit * (1 - have if d & bit else have)
        bit *= 2
    return out


def remote(src, dst, send, recv, to):
    return pltpu.make_async_remote_copy(
        src_ref=src, dst_ref=dst, send_sem=send, recv_sem=recv, device_id=to, device_id_type=MESH
    )


def greet(targets):
    barrier = pltpu.get_barrier_semaphore()
    for to in targets:
        pl.semaphore_signal(barrier, inc=1, device_id=to, device_id_type=MESH)
    pl.semaphore_wait(barrier, len(targets))


def places(n_ops, n_blk):
    g, c = lax.axis_index("ops"), lax.axis_index("blk")
    chips = n_ops // 2
    z, core = g // 2, g % 2
    peers = [across(c, d, n_blk) for d in range(n_blk)]
    up = [((z + e) % chips) * 2 + core for e in range(chips)]
    down = [((z + chips - e) % chips) * 2 + core for e in range(chips)]
    partner = z * 2 + (1 - core)
    return g, c, z, core, peers, up, down, partner


def shares(my_rows, n_ops):
    piece = max(my_rows * 3 // 4 // n_ops // 16, 1) * 16
    return piece, (my_rows - piece * n_ops) // 2


def gather_kernel(
    n_ops, n_blk, psi_ref, left_ref, pair_ref, psi_out, left_out, stage,
    send_a, recv_a, send_l, recv_l, send_c, recv_c, send_z, recv_z, send_p, recv_p,
):
    g, c, z, core, peers, up, down, partner = places(n_ops, n_blk)
    chips = n_ops // 2
    piece, straight = shares(psi_ref.shape[0], n_ops)
    group = left_ref.shape[0]
    local_ops = group // n_blk

    def rows_of(chip, which):
        return pl.ds(pl.multiple_of((chip * 2 + which) * piece, piece), piece)

    def straight_of(which):
        return pl.ds(pl.multiple_of(piece * n_ops + which * straight, 16), straight)

    greet(
        [(g, peers[d]) for d in range(1, n_blk)]
        + [(up[1], c), (down[1], c), (partner, c)]
    )
    order = list(range(1, n_blk))
    mine = rows_of(z, core)
    first = {
        d: remote(psi_ref.at[mine], psi_out.at[c, mine], send_a.at[d], recv_a.at[d], (g, peers[d]))
        for d in order
    }
    for d in order:
        first[d].start()
    for j in range(group):
        stage[j] = left_ref[lax.rem(pair_ref[j], group)]
    lefts = {
        d: remote(
            stage.at[pl.ds(peers[d] * local_ops, local_ops)],
            left_out.at[c], send_l.at[d], recv_l.at[d], (g, peers[d]),
        )
        for d in order
    }
    at = straight_of(core) if straight else None
    plain = {
        d: remote(psi_ref.at[at], psi_out.at[c, at], send_c.at[d], recv_c.at[d], (g, peers[d]))
        for d in order if straight
    }
    for d in order:
        if straight:
            plain[d].start()
    for d in order:
        lefts[d].start()
    psi_out[c] = psi_ref[...]
    left_out[c] = stage[pl.ds(c * local_ops, local_ops)]

    def hop(d, h, way, source):
        here = psi_out.at[peers[d], rows_of(source, core)]
        to = (g + 2, c) if way == 0 else (g - 2, c)
        return remote(here, here, send_z.at[way, d, h], recv_z.at[way, d, h], to)

    def share(d, h, way, source, which):
        here = psi_out.at[peers[d], rows_of(source, which)]
        return remote(here, here, send_p.at[way, d, h], recv_p.at[way, d, h], (partner, c))

    def can_send(h, way):
        if way == 0:
            return jnp.logical_and(z >= h, z < chips - 1)
        return jnp.logical_and(z < chips - h, z > 0)

    def has(h, way):
        return z >= h if way == 0 else z < chips - h

    def source_of(h, way):
        return z - h if way == 0 else z + h

    for h in range(chips):
        for d in order:
            if h == 0:
                first[d].wait_recv()
                share(d, 0, 0, z, core).start()
            for way in range(2):
                source = source_of(h, way)
                if h:
                    @pl.when(has(h, way))
                    def _(d=d, h=h, way=way, source=source):
                        hop(d, h - 1, way, source).wait_recv()
                        share(d, h, way, source, core).start()
                if h < chips - 1:
                    @pl.when(can_send(h, way))
                    def _(d=d, h=h, way=way, source=source):
                        hop(d, h, way, source).start()
    for d in order if straight else []:
        plain[d].wait_recv()
        here = psi_out.at[peers[d], at]
        remote(here, here, send_c.at[d + n_blk], recv_c.at[d + n_blk], (partner, c)).start()
    for d in order:
        if straight:
            here = psi_out.at[peers[d], straight_of(1 - core)]
            remote(here, here, send_c.at[d + n_blk], recv_c.at[d + n_blk], (partner, c)).wait()
            plain[d].wait_send()
        lefts[d].wait()
        first[d].wait_send()
        share(d, 0, 0, z, 1 - core).wait()
        for way in range(2):
            for h in range(chips):
                source = source_of(h, way)
                if h:
                    @pl.when(has(h, way))
                    def _(d=d, h=h, way=way, source=source):
                        share(d, h, way, source, 1 - core).wait()
                if h < chips - 1:
                    @pl.when(can_send(h, way))
                    def _(d=d, h=h, way=way, source=source):
                        hop(d, h, way, source).wait_send()


def mix_kernel(target_ref, pair_ref, len_ref, psi_ref, left_ref, out_ref, total):
    blocks, block_rows, columns = psi_ref.shape
    local_ops = total.shape[0]
    per = left_ref.shape[2]
    group = target_ref.shape[0]
    c = lax.axis_index("blk")
    total[...] = jnp.zeros_like(total)
    lane = lax.broadcasted_iota(jnp.int32, (1, block_rows), 1)
    row = lax.broadcasted_iota(jnp.int32, (block_rows, 1), 0)
    owners = [lax.rem(pair_ref[c * local_ops + r], group) for r in range(local_ops)]

    def one(q, carry):
        left = left_ref[q // per, :, q % per].reshape(local_ops * block_rows, block_rows)
        left = jnp.where(lane < len_ref[q], left, jnp.zeros_like(left))
        mixed = jnp.dot(left, psi_ref[q], preferred_element_type=jnp.float32)
        for r in range(local_ops):
            total[r, target_ref[owners[r], q]] += mixed[r * block_rows : (r + 1) * block_rows]
        return carry

    lax.fori_loop(0, blocks, one, 0, unroll=4)

    def out(t, carry):
        for r in range(local_ops):
            kept = total[r, t]
            kept = jnp.where(row < len_ref[t], kept, jnp.zeros_like(kept))
            out_ref[r, t] = kept.astype(out_ref.dtype)
        return carry

    lax.fori_loop(0, blocks, out, 0)


def reduce_kernel(
    n_ops, n_blk, y_hbm, r_hbm, out_ref,
    y_v, r_v, part, recv1, send2, recv2, send3, recv3,
    y_sem, r_sem, send_1, recv_1, send_2, recv_2, send_3, recv_3,
):
    g, c, z, core, peers, up, down, partner = places(n_ops, n_blk)
    chips = n_ops // 2
    local_ops = r_hbm.shape[0]
    rows = y_v.shape[2]
    thin = out_ref.shape[1]
    wide = 2 * thin
    order = list(range(n_blk - 1, -1, -1))

    def load(d):
        at = pl.ds(pl.multiple_of(peers[d] * rows, rows), rows)
        return pltpu.make_async_copy(y_hbm.at[:, at], y_v.at[d], y_sem.at[d])

    def weights(k):
        j = (z + 1 + k) % chips
        cols = pl.ds(pl.multiple_of(j * wide, wide), wide)
        return pltpu.make_async_copy(r_hbm.at[:, :, cols], r_v.at[k], r_sem.at[k])

    weights(0).start()
    for d in order:
        load(d).start()
    for k in range(1, chips):
        weights(k).start()
    greet(
        [(g, peers[d]) for d in range(1, n_blk)]
        + [(up[e], c) for e in range(1, chips)]
        + [(partner, c)]
    )

    def product(k, d):
        acc = jnp.dot(y_v[d, 0], r_v[k, 0], preferred_element_type=jnp.float32)
        for r in range(1, local_ops):
            acc += jnp.dot(y_v[d, r], r_v[k, r], preferred_element_type=jnp.float32)
        acc = acc.astype(jnp.bfloat16)
        part[k, 0, d] = acc[:, :thin]
        part[k, 1, d] = acc[:, thin:]

    def swap(k):
        return remote(
            part.at[k, 1 - core], recv1.at[k], send_1.at[k], recv_1.at[k], (partner, c)
        )

    def spread(k, d):
        return remote(
            send2.at[k, d], recv2.at[k, d], send_2.at[k, d], recv_2.at[k, d], (g, peers[d])
        )

    def last(k):
        return remote(
            send3.at[k], recv3.at[k], send_3.at[k], recv_3.at[k], (up[k + 1], c)
        )

    def compute(k):
        weights(k).wait()
        if k == 0:
            for d in order:
                load(d).wait()
                product(k, d)
        else:
            lax.fori_loop(0, n_blk, lambda d, carry: (product(k, d), carry)[1], 0)
        swap(k).start()

    def join(k):
        swap(k).wait_recv()
        for d in order:
            send2[k, d] = (
                part[k, core, d].astype(jnp.float32) + recv1[k, d].astype(jnp.float32)
            ).astype(jnp.bfloat16)
            if d:
                spread(k, d).start()

    def finish(k):
        acc = send2[k, 0].astype(jnp.float32)
        for d in range(1, n_blk):
            spread(k, d).wait_recv()
            acc += recv2[k, d].astype(jnp.float32)
        if k < chips - 1:
            send3[k] = acc.astype(jnp.bfloat16)
            last(k).start()
            return
        for e in range(chips - 1):
            last(e).wait_recv()
            acc += recv3[e].astype(jnp.float32)
        out_ref[...] = acc.astype(out_ref.dtype)

    compute(0)
    for k in range(1, chips):
        compute(k)
        join(k - 1)
        if k > 2:
            finish(k - 3)
    join(chips - 1)
    for k in range(max(chips - 3, 0), chips):
        finish(k)
    for k in range(chips):
        swap(k).wait_send()
        for d in range(1, n_blk):
            spread(k, d).wait_send()
        if k < chips - 1:
            last(k).wait_send()


def local(n_ops, n_blk, psi, left_blocks, right_ops, block_target, left_partner, block_len):
    group, local_blocks, block_rows, _ = left_blocks.shape
    my_rows, columns = psi.shape
    local_ops = right_ops.shape[0]
    blocks = block_target.shape[1]
    chips = n_ops // 2
    thin = columns // n_ops
    bf16 = jnp.bfloat16
    in_vmem = pl.BlockSpec(memory_space=pltpu.VMEM)
    in_smem = pl.BlockSpec(memory_space=pltpu.SMEM)
    in_hbm = pl.BlockSpec(memory_space=pl.ANY)

    psi_all, left_all = pl.pallas_call(
        functools.partial(gather_kernel, n_ops, n_blk),
        out_shape=(
            jax.ShapeDtypeStruct((n_blk, my_rows, columns), bf16),
            jax.ShapeDtypeStruct((n_blk, local_ops, local_blocks, block_rows, block_rows), bf16),
        ),
        in_specs=[in_vmem, in_vmem, in_smem],
        out_specs=(in_vmem, in_vmem),
        scratch_shapes=[
            VMEM(left_blocks.shape, bf16),
            DMA((n_blk,)), DMA((n_blk,)), DMA((n_blk,)), DMA((n_blk,)),
            DMA((2 * n_blk,)), DMA((2 * n_blk,)),
            DMA((2, n_blk, chips)), DMA((2, n_blk, chips)),
            DMA((2, n_blk, chips)), DMA((2, n_blk, chips)),
        ],
        compiler_params=pltpu.CompilerParams(collective_id=0, has_side_effects=True),
        name="gather",
    )(psi, left_blocks, left_partner)

    step = min(columns, 256)
    mixed = pl.pallas_call(
        mix_kernel,
        grid=(columns // step,),
        out_shape=jax.ShapeDtypeStruct((local_ops, blocks, block_rows, columns), bf16),
        in_specs=[
            in_smem, in_smem, in_smem,
            pl.BlockSpec((blocks, block_rows, step), lambda i: (0, 0, i)),
            pl.BlockSpec(left_all.shape, lambda i: (0,) * 5),
        ],
        out_specs=pl.BlockSpec((local_ops, blocks, block_rows, step), lambda i: (0, 0, 0, i)),
        scratch_shapes=[VMEM((local_ops, blocks, block_rows, step), jnp.float32)],
        compiler_params=pltpu.CompilerParams(vmem_limit_bytes=63 * 2**20),
        name="mix",
    )(
        block_target, left_partner, block_len,
        psi_all.reshape(blocks, block_rows, columns), left_all,
    )

    return pl.pallas_call(
        functools.partial(reduce_kernel, n_ops, n_blk),
        out_shape=jax.ShapeDtypeStruct((my_rows, thin), bf16),
        in_specs=[in_hbm, in_hbm],
        out_specs=in_vmem,
        scratch_shapes=[
            VMEM((n_blk, local_ops, my_rows, columns), bf16),
            VMEM((chips, local_ops, columns, 2 * thin), bf16),
            VMEM((chips, 2, n_blk, my_rows, thin), bf16),
            VMEM((chips, n_blk, my_rows, thin), bf16),
            VMEM((chips, n_blk, my_rows, thin), bf16),
            VMEM((chips, n_blk, my_rows, thin), bf16),
            VMEM((chips, my_rows, thin), bf16),
            VMEM((chips, my_rows, thin), bf16),
            DMA((n_blk,)), DMA((chips,)), DMA((chips,)), DMA((chips,)),
            DMA((chips, n_blk)), DMA((chips, n_blk)), DMA((chips,)), DMA((chips,)),
        ],
        compiler_params=pltpu.CompilerParams(
            collective_id=1, has_side_effects=True, vmem_limit_bytes=63 * 2**20
        ),
        name="reduce",
    )(mixed.reshape(local_ops, blocks * block_rows, columns), right_ops)


def solution(mesh):
    return jax.shard_map(
        functools.partial(local, mesh.shape["ops"], mesh.shape["blk"]),
        mesh=mesh,
        in_specs=(
            P("blk", None),
            P("ops", "blk", None, None),
            P(("ops", "blk"), None, None),
            P("ops", None),
            P("ops"),
            P(),
        ),
        out_specs=P("blk", "ops"),
        check_vma=False,
    )
```

profile of v0, /device:TPU:0, one launch (start us, length us, event | category | flops | bytes accessed | tf_op | source)
XLA Modules:
  0.0 83.4 jit_solution(4637055168566520700)
XLA Ops:
  0.0 35.0 %gather.1 = (bf16[4,512,1024]{2,1,0:T(8,128)(2,1)}, bf16[4,2,4,128,128]{4,3,2,1,0:T(8,128)(2,1)}) custom-call(bf16[512,1024]{1,0:T(8,128)(2,1)} %psi_ref.1, bf16[8,4,128,128]{3,2,1,0:T(8,128)(2,1)} %left_ref.1, s32[8]{0:T(128)} %pair_ref.3), custom_call_target="tpu_custom_call" | custom-call | tf_op jit(solution)/shard_map/gather/pallas_call | solution.py:313
  35.0 10.8 %mix.1 = bf16[2,16,128,1024]{3,2,1,0:T(8,128)(2,1)} custom-call(s32[8,16]{1,0:T(8,128)} %target_ref.1, s32[8]{0:T(128)} %pair_ref.3, s32[16]{0:T(128)} %len_ref.1, bf16[16,128,1024]{2,1,0:T(8,128)(2,1)} %bitcast.3, bf16[4,2,4,128,128]{4,3,2,1,0:T(8,128)(2,1)} %get-tuple-element.8.left_ref), custom_call_target="tpu_custom_call" | custom-call | tf_op jit(solution)/shard_map/mix/pallas_call | solution.py:333
  45.8 36.0 %reduce.1 = bf16[512,128]{1,0:T(8,128)(2,1)} custom-call(bf16[2,2048,1024]{2,1,0:T(8,128)(2,1)} %bitcast.2, bf16[2,1024,1024]{2,1,0:T(8,128)(2,1)} %r_hbm.1), custom_call_target="tpu_custom_call" | custom-call | tf_op jit(solution)/shard_map/reduce/pallas_call | solution.py:351
  81.9 1.6 %copy.8 = bf16[512,128]{1,0:T(8,128)(2,1)} copy(bf16[512,128]{1,0:T(8,128)(2,1)} %reduce.1) | data formatting | bytes 262144
where the time goes:
time: 83.7 us; the launch traced here: 83.4 us
  Pallas kernels  81.9 us (98%)
  local copies, waits for them, and re-layouts  1.57 us (2%)
    pallas_call x1, Pallas kernels, local(): pl.pallas_call(functools.partial(reduce_kernel, n_ops, n_blk), out_shape=...  36 us
    pallas_call x1, Pallas kernels, local(): pl.pallas_call(functools.partial(gather_kernel, n_ops, n_blk), out_shape=...  35 us
    pallas_call x1, Pallas kernels, local(): pl.pallas_call(mix_kernel, grid=(columns // step,), out_shape=jax.ShapeDt...  10.8 us

commit v1 on v0

v1 whole, which is shorter than its diff:
```python
import functools

import jax
import jax.numpy as jnp
from jax import lax
from jax.experimental import pallas as pl
from jax.experimental.pallas import tpu as pltpu
from jax.sharding import PartitionSpec as P

MESH = pl.DeviceIdType.MESH
VMEM = pltpu.VMEM
SMEM = pltpu.SMEM
DMA = pltpu.SemaphoreType.DMA
F32 = jnp.float32
BF16 = jnp.bfloat16


def across(c, d, n):
    out, bit = 0, 1
    while bit < n:
        out = out + bit * ((c // bit + d // bit) % 2)
        bit *= 2
    return out


def remote(src, dst, send, recv, to):
    return pltpu.make_async_remote_copy(
        src_ref=src, dst_ref=dst, send_sem=send, recv_sem=recv, device_id=to, device_id_type=MESH
    )


def greet(targets):
    barrier = pltpu.get_barrier_semaphore()
    for to in targets:
        pl.semaphore_signal(barrier, inc=1, device_id=to, device_id_type=MESH)
    pl.semaphore_wait(barrier, len(targets))


def shares(half_rows, chips):
    piece = max(half_rows * 3 // 4 // chips // 16, 1) * 16
    return piece, half_rows - piece * chips


def sigma_kernel(
    n_ops, n_blk, psi_hbm, left_hbm, r_hbm, target_ref, pair_ref, len_ref, out_ref,
    psi_v, left_in, stage, left_v, r_v, img, run, tab_v, tab_s, prev_s, last_s,
    part, recv1, sum1, recv_a1, recv_b1, send_a2, recv_a2, send_b2, recv_b2, send3, recv3,
    s_load, s_r, ss_a, sr_a, ss_c, sr_c, ss_l, sr_l, ss_z, sr_z, ss_y, ss_r, sr_r, ss_t, sr_t,
    ss_1, sr_1, ss_a1, sr_a1, ss_b1, sr_b1, ss_a2, sr_a2, ss_b2, sr_b2, ss_3, sr_3,
):
    g, c = lax.axis_index("ops"), lax.axis_index("blk")
    chips = n_ops // 2
    z, core = g // 2, g % 2
    partner = (z * 2 + (1 - core), c)
    peers = [across(c, d, n_blk) for d in range(n_blk)]
    order = list(range(1, n_blk))
    others = sorted(range(1, chips), key=lambda e: (abs(e * 2 - chips), e))

    half_rows, columns = psi_v.shape[1:]
    group, local_blocks, block_rows, _ = left_in.shape
    half_blocks = local_blocks // 2
    local_ops = r_hbm.shape[0]
    blocks = target_ref.shape[1]
    pairs = run.shape[0] - 1
    wide = r_v.shape[4]
    thin = wide // 2
    rest = n_blk // 2
    piece, straight = shares(half_rows, chips)

    def at_chip(e):
        return lax.rem(z + e, chips)

    mine = pl.ds(pl.multiple_of(core * half_rows, half_rows), half_rows)
    get_psi = pltpu.make_async_copy(psi_hbm.at[mine], psi_v.at[0], s_load.at[0])
    get_left = pltpu.make_async_copy(left_hbm, left_in, s_load.at[1])

    def get_r(j):
        return pltpu.make_async_copy(
            r_hbm.at[:, :, pl.ds(j * wide, wide)], r_v.at[0, j], s_r.at[j]
        )

    get_psi.start()
    get_left.start()
    for j in range(chips):
        get_r(j).start()

    greet(
        [partner]
        + [(z * 2 + k, peers[d]) for d in order for k in range(2)]
        + [(at_chip(e) * 2 + core, c) for e in range(1, chips)]
    )

    def rows_of(chip):
        return pl.ds(pl.multiple_of(chip * piece, piece), piece)

    rest_rows = pl.ds(piece * chips, straight)

    def first(d):
        return remote(
            psi_v.at[0, rows_of(z)], psi_v.at[d, rows_of(z)], ss_a.at[d], sr_a.at[d], (g, peers[d])
        )

    def plain(d):
        return remote(
            psi_v.at[0, rest_rows], psi_v.at[d, rest_rows], ss_c.at[d], sr_c.at[d], (g, peers[d])
        )

    def along(d, e):
        here = psi_v.at[d, rows_of(z)]
        return remote(here, here, ss_z.at[d, e], sr_z.at[d, z], (at_chip(e) * 2 + core, c))

    def passed(d, way):
        source, to = (0, chips - 1) if way == 0 else (chips - 1, 0)
        here = psi_v.at[d, rows_of(source)]
        return remote(here, here, ss_y.at[d, way], sr_z.at[d, source], (to * 2 + core, c))

    def arrived(d, source):
        here = psi_v.at[d, rows_of(source)]
        return remote(here, here, ss_z.at[d, 0], sr_z.at[d, source], partner)

    relay = chips > 2

    def near(e):
        if not relay:
            return True
        to = at_chip(e)
        return jnp.logical_and(to - z < chips - 1, z - to < chips - 1)

    def relays(way):
        return z == (chips - 2 if way == 0 else 1)

    def swap_r(j):
        return remote(r_v.at[0, j], r_v.at[1, j], ss_r.at[j], sr_r.at[j], partner)

    def lefts(d, k):
        which = core if k == 0 else 1 - core
        to = (z * 2 + which, peers[d])
        first_op = pl.multiple_of(peers[d] * local_ops, local_ops)
        return remote(
            stage.at[which, pl.ds(first_op, local_ops)], left_v.at[d, k],
            ss_l.at[d, k], sr_l.at[d, k], to,
        )

    table = remote(tab_v.at[0], tab_v.at[1], ss_t, sr_t, partner)

    get_psi.wait()
    for d in order:
        first(d).start()
    for d in order:
        if straight:
            plain(d).start()

    tab_v[0] = jnp.zeros_like(tab_v[0])
    for j in range(group):
        tab_v[0, j : j + 1, :blocks] = target_ref[pl.ds(lax.rem(pair_ref[j], group), 1), :]
    table.start()

    get_left.wait()
    lane = lax.broadcasted_iota(jnp.int32, (1, block_rows), 1)

    def put(j, carry):
        owner = lax.rem(pair_ref[j], group)
        for k in range(2):
            for i in range(half_blocks):
                b = k * half_blocks + i
                live = lane < len_ref[c * local_blocks + b]
                block = left_in[owner, b]
                stage[k, j, i] = jnp.where(live, block, jnp.zeros_like(block))
        return carry

    lax.fori_loop(0, group, put, 0)
    for d in order:
        for k in range(2):
            lefts(d, k).start()
    for j in range(chips):
        get_r(j).wait()
        swap_r(j).start()
    lefts(0, 1).start()
    left_v[0, 0] = stage[core, pl.ds(c * local_ops, local_ops)]
    run[pairs] = jnp.zeros_like(run[pairs])

    def image(d, k):
        def one(j, carry):
            for r in range(local_ops):
                out = jnp.dot(psi_v[d], r_v[k, j, r], preferred_element_type=F32)
                img[j, d, k, r] = out.astype(BF16).reshape(half_blocks, block_rows, wide)
            return carry

        lax.fori_loop(0, chips, one, 0)

    image(0, 0)
    for d in order:
        first(d).wait_recv()
        for e in others:
            @pl.when(near(e))
            def _(d=d, e=e):
                along(d, e).start()

    table.wait_recv()
    get_table = pltpu.make_async_copy(tab_v, tab_s, s_load.at[2])
    get_table.start()
    get_table.wait()

    def link(p, last):
        i = p % half_blocks
        r = p // half_blocks % local_ops
        k = p // (half_blocks * local_ops) % 2
        d = p // (half_blocks * local_ops * 2)
        q = across(c, d, n_blk) * local_blocks + core * half_blocks + i
        t = tab_s[k, c * local_ops + r, q]
        before = jnp.int32(pairs)
        for b in range(blocks):
            before = jnp.where(t == b, last[b], before)
        prev_s[p] = before
        return tuple(jnp.where(t == b, p, last[b]) for b in range(blocks))

    last = lax.fori_loop(0, pairs, link, (jnp.int32(pairs),) * blocks)
    for b in range(blocks):
        last_s[b] = last[b]

    def pass_on(d):
        for way in range(2 if relay else 0):
            @pl.when(relays(way))
            def _(way=way):
                arrived(d, 0 if way == 0 else chips - 1).wait_recv()
                passed(d, way).start()

    def settle(d):
        for e in range(1, chips):
            source = at_chip(e)
            done = False
            if relay:
                done = jnp.logical_or(
                    jnp.logical_and(relays(0), source == 0),
                    jnp.logical_and(relays(1), source == chips - 1),
                )

            @pl.when(jnp.logical_not(done))
            def _(source=source):
                arrived(d, source).wait_recv()
        if straight:
            plain(d).wait_recv()

    pass_on(1)
    for j in range(chips):
        swap_r(j).wait_recv()
    image(0, 1)
    for d in order:
        if d + 1 < n_blk:
            pass_on(d + 1)
        settle(d)
        for k in range(2):
            image(d, k)
    lefts(0, 1).wait_recv()
    for d in order:
        for k in range(2):
            lefts(d, k).wait_recv()

    def mix(n):
        j = at_chip(n + 1)

        def one(p, carry):
            i = p % half_blocks
            r = p // half_blocks % local_ops
            k = p // (half_blocks * local_ops) % 2
            d = p // (half_blocks * local_ops * 2)
            mixed = jnp.dot(left_v[d, k, r, i], img[j, d, k, r, i], preferred_element_type=F32)
            run[p] = run[prev_s[p]] + mixed
            return carry

        lax.fori_loop(0, pairs, one, 0, unroll=4)

        def emit(d, carry):
            for i in range(local_blocks):
                half, at = i // half_blocks, i % half_blocks
                slot = d % 2 * rest + d // 2 if half == 0 else d
                rows = pl.ds(at * block_rows, block_rows)
                kept = run[last_s[across(c, d, n_blk) * local_blocks + i]].astype(BF16)
                part[n, 0, half, slot, rows] = kept[:, :thin]
                part[n, 1, half, slot, rows] = kept[:, thin:]
            return carry

        lax.fori_loop(0, n_blk, emit, 0)
        swap(n).start()

    def swap(n):
        return remote(part.at[n, 1 - core], recv1.at[n], ss_1.at[n], sr_1.at[n], partner)

    def step_a1(n):
        return remote(
            sum1.at[n, 0, pl.ds(rest, rest)], recv_a1.at[n], ss_a1.at[n], sr_a1.at[n], (g, peers[1])
        )

    def step_b1(n, dy):
        return remote(
            sum1.at[n, 1, pl.ds(2 * dy, 2)], recv_b1.at[n, dy],
            ss_b1.at[n, dy], sr_b1.at[n, dy], (g, peers[2 * dy]),
        )

    def step_a2(n, dy):
        return remote(
            send_a2.at[n, dy], recv_a2.at[n, dy], ss_a2.at[n, dy], sr_a2.at[n, dy], (g, peers[2 * dy])
        )

    def step_b2(n):
        return remote(send_b2.at[n], recv_b2.at[n], ss_b2.at[n], sr_b2.at[n], (g, peers[1]))

    def last_step(n):
        return remote(
            send3.at[n], recv3.at[n], ss_3.at[n], sr_3.at[n], (at_chip(n + 1) * 2 + core, c)
        )

    def join(n):
        swap(n).wait_recv()

        def add(half, slots):
            both = part[n, core, half, slots].astype(F32) + recv1[n, half, slots].astype(F32)
            sum1[n, half, slots] = both.astype(BF16)

        add(0, pl.ds(rest, rest))
        step_a1(n).start()
        add(1, pl.ds(2, n_blk - 2))
        for dy in range(1, rest):
            step_b1(n, dy).start()
        add(0, pl.ds(0, rest))
        add(1, pl.ds(0, 2))

    def middle(n):
        step_a1(n).wait_recv()
        for dy in range(1, rest):
            both = sum1[n, 0, dy].astype(F32) + recv_a1[n, dy].astype(F32)
            send_a2[n, dy] = both.astype(BF16)
            step_a2(n, dy).start()
        both = sum1[n, 1, 1].astype(F32)
        for dy in range(1, rest):
            step_b1(n, dy).wait_recv()
            both += recv_b1[n, dy, 1].astype(F32)
        send_b2[n] = both.astype(BF16)
        step_b2(n).start()

    def finish(n):
        a = sum1[n, 0, 0].astype(F32) + recv_a1[n, 0].astype(F32)
        b = sum1[n, 1, 0].astype(F32)
        for dy in range(1, rest):
            step_a2(n, dy).wait_recv()
            a += recv_a2[n, dy].astype(F32)
            b += recv_b1[n, dy, 0].astype(F32)
        step_b2(n).wait_recv()
        b += recv_b2[n].astype(F32)
        if n < chips - 1:
            send3[n, 0] = a.astype(BF16)
            send3[n, 1] = b.astype(BF16)
            last_step(n).start()
            return
        for e in range(chips - 1):
            last_step(e).wait_recv()
            a += recv3[e, 0].astype(F32)
            b += recv3[e, 1].astype(F32)
        row = lax.broadcasted_iota(jnp.int32, (block_rows, 1), 0)
        for i in range(local_blocks):
            at = i % half_blocks * block_rows
            kept = (a if i < half_blocks else b)[at : at + block_rows]
            kept = jnp.where(row < len_ref[c * local_blocks + i], kept, jnp.zeros_like(kept))
            out_ref[i * block_rows : (i + 1) * block_rows] = kept.astype(out_ref.dtype)

    for n in range(chips + 3):
        if n < chips:
            mix(n)
        if 0 <= n - 1 < chips:
            join(n - 1)
        if 0 <= n - 2 < chips:
            middle(n - 2)
        if 0 <= n - 3 < chips:
            finish(n - 3)

    table.wait_send()
    lefts(0, 1).wait_send()
    for j in range(chips):
        swap_r(j).wait_send()
    for d in order:
        first(d).wait_send()
        if straight:
            plain(d).wait_send()
        for k in range(2):
            lefts(d, k).wait_send()
        for e in others:
            @pl.when(near(e))
            def _(d=d, e=e):
                along(d, e).wait_send()
        for way in range(2 if relay else 0):
            @pl.when(relays(way))
            def _(d=d, way=way):
                passed(d, way).wait_send()
    for n in range(chips):
        swap(n).wait_send()
        step_a1(n).wait_send()
        step_b2(n).wait_send()
        for dy in range(1, rest):
            step_b1(n, dy).wait_send()
            step_a2(n, dy).wait_send()
        if n < chips - 1:
            last_step(n).wait_send()


def local(n_ops, n_blk, psi, left_blocks, right_ops, block_target, left_partner, block_len):
    group, local_blocks, block_rows, _ = left_blocks.shape
    my_rows, columns = psi.shape
    local_ops = right_ops.shape[0]
    blocks = block_target.shape[1]
    chips = n_ops // 2
    thin = columns // n_ops
    wide = 2 * thin
    half_rows, half_blocks = my_rows // 2, local_blocks // 2
    rest = n_blk // 2
    pairs = n_blk * 2 * local_ops * half_blocks
    in_vmem = pl.BlockSpec(memory_space=pltpu.VMEM)
    in_smem = pl.BlockSpec(memory_space=pltpu.SMEM)
    in_hbm = pl.BlockSpec(memory_space=pl.ANY)

    def dmas(*shapes):
        return [DMA(shape) for shape in shapes for _ in range(2)]

    return pl.pallas_call(
        functools.partial(sigma_kernel, n_ops, n_blk),
        out_shape=jax.ShapeDtypeStruct((my_rows, thin), BF16),
        in_specs=[in_hbm, in_hbm, in_hbm, in_vmem, in_smem, in_smem],
        out_specs=in_vmem,
        scratch_shapes=[
            VMEM((n_blk, half_rows, columns), BF16),
            VMEM(left_blocks.shape, BF16),
            VMEM((2, group, half_blocks, block_rows, block_rows), BF16),
            VMEM((n_blk, 2, local_ops, half_blocks, block_rows, block_rows), BF16),
            VMEM((2, chips, local_ops, columns, wide), BF16),
            VMEM((chips, n_blk, 2, local_ops, half_blocks, block_rows, wide), BF16),
            VMEM((pairs + 1, block_rows, wide), F32),
            VMEM((2, group, 128), jnp.int32),
            SMEM((2, group, 128), jnp.int32),
            SMEM((pairs,), jnp.int32),
            SMEM((blocks,), jnp.int32),
            VMEM((chips, 2, 2, n_blk, half_rows, thin), BF16),
            VMEM((chips, 2, n_blk, half_rows, thin), BF16),
            VMEM((chips, 2, n_blk, half_rows, thin), BF16),
            VMEM((chips, rest, half_rows, thin), BF16),
            VMEM((chips, rest, 2, half_rows, thin), BF16),
            VMEM((chips, rest, half_rows, thin), BF16),
            VMEM((chips, rest, half_rows, thin), BF16),
            VMEM((chips, half_rows, thin), BF16),
            VMEM((chips, half_rows, thin), BF16),
            VMEM((chips, 2, half_rows, thin), BF16),
            VMEM((chips, 2, half_rows, thin), BF16),
            DMA((3,)), DMA((chips,)),
            *dmas((n_blk,), (n_blk,), (n_blk, 2), (n_blk, chips)),
            DMA((n_blk, 2)),
            *dmas((chips,), ()),
            *dmas((chips,), (chips,), (chips, rest), (chips, rest), (chips,), (chips,)),
        ],
        compiler_params=pltpu.CompilerParams(
            collective_id=0, has_side_effects=True, vmem_limit_bytes=63 * 2**20
        ),
        name="sigma",
    )(psi, left_blocks, right_ops, block_target, left_partner, block_len)


def solution(mesh):
    return jax.shard_map(
        functools.partial(local, mesh.shape["ops"], mesh.shape["blk"]),
        mesh=mesh,
        in_specs=(
            P("blk", None),
            P("ops", "blk", None, None),
            P(("ops", "blk"), None, None),
            P("ops", None),
            P("ops"),
            P(),
        ),
        out_specs=P("blk", "ops"),
        check_vma=False,
    )
```

time: 83.7 us -> 65.4 us (0.78)
  Pallas kernels: 81.9 us -> 63.6 us
    pallas_call x3 -> x1, Pallas kernels: 81.9 us -> 63.6 us  [local(): pl.pallas_call(functools.partial(sigma_kernel, n_ops, n_blk), out_shape=j...]
where the time goes in v1:
time: 65.4 us; the launch traced here: 65.2 us
  Pallas kernels  63.6 us (97%)
  local copies, waits for them, and re-layouts  1.57 us (2%)
    pallas_call x1, Pallas kernels, local(): pl.pallas_call(functools.partial(sigma_kernel, n_ops, n_blk), out_shape=j...  63.6 us
    unnamed x1, local copies, waits for them, and re-layouts  1.57 us

profile of v1, /device:TPU:0, one launch (start us, length us, event | category | flops | bytes accessed | tf_op | source)
XLA Modules:
  0.0 65.2 jit_solution(6584733584137062281)
XLA Ops:
  0.0 63.6 %sigma.1 = bf16[512,128]{1,0:T(8,128)(2,1)} custom-call(bf16[512,1024]{1,0:T(8,128)(2,1)} %psi_hbm.1, bf16[8,4,128,128]{3,2,1,0:T(8,128)(2,1)} %left_hbm.1, bf16[2,1024,1024]{2,1,0:T(8,128)(2,1)} %r_hbm.1, s32[8,16]{1,0:T(8,128)} %target_ref.1, s32[8]{0:T(128)} %pair_ref.1, s32[16]{0:T(128)} %len_ref.1), custom_call_target="tpu_custom_call" | custom-call | tf_op jit(solution)/shard_map/sigma/pallas_call | solution.py:423
  63.6 1.6 %copy.8 = bf16[512,128]{1,0:T(8,128)(2,1)} copy(bf16[512,128]{1,0:T(8,128)(2,1)} %sigma.1) | data formatting | bytes 262144

commit v2 on v1

--- a/solution.py
+++ b/solution.py
@@ -13,6 +13,7 @@
 DMA = pltpu.SemaphoreType.DMA
 F32 = jnp.float32
 BF16 = jnp.bfloat16
+scope = jax.named_scope
 
 
 def across(c, d, n):
@@ -29,23 +30,16 @@
     )
 
 
-def greet(targets):
-    barrier = pltpu.get_barrier_semaphore()
-    for to in targets:
-        pl.semaphore_signal(barrier, inc=1, device_id=to, device_id_type=MESH)
-    pl.semaphore_wait(barrier, len(targets))
-
-
 def shares(half_rows, chips):
-    piece = max(half_rows * 3 // 4 // chips // 16, 1) * 16
-    return piece, half_rows - piece * chips
+    sizes = [max(half_rows // 2 // chips // 16, 1) * 16] * chips
+    return sizes, [sum(sizes[:n]) for n in range(chips)]
 
 
 def sigma_kernel(
     n_ops, n_blk, psi_hbm, left_hbm, r_hbm, target_ref, pair_ref, len_ref, out_ref,
     psi_v, left_in, stage, left_v, r_v, img, run, tab_v, tab_s, prev_s, last_s,
     part, recv1, sum1, recv_a1, recv_b1, send_a2, recv_a2, send_b2, recv_b2, send3, recv3,
-    s_load, s_r, ss_a, sr_a, ss_c, sr_c, ss_l, sr_l, ss_z, sr_z, ss_y, ss_r, sr_r, ss_t, sr_t,
+    s_load, s_r, ss_a, sr_a, ss_c, sr_c, ss_f, sr_f, ss_g, sr_g, ss_l, sr_l, ss_z, sr_z, ss_y, above, ss_r, sr_r, ss_t, sr_t,
     ss_1, sr_1, ss_a1, sr_a1, ss_b1, sr_b1, ss_a2, sr_a2, ss_b2, sr_b2, ss_3, sr_3,
 ):
     g, c = lax.axis_index("ops"), lax.axis_index("blk")
@@ -54,50 +48,67 @@
     partner = (z * 2 + (1 - core), c)
     peers = [across(c, d, n_blk) for d in range(n_blk)]
     order = list(range(1, n_blk))
-    others = sorted(range(1, chips), key=lambda e: (abs(e * 2 - chips), e))
 
     half_rows, columns = psi_v.shape[1:]
     group, local_blocks, block_rows, _ = left_in.shape
     half_blocks = local_blocks // 2
     local_ops = r_hbm.shape[0]
+    thin = out_ref.shape[1]
+    wide = 2 * thin
     blocks = target_ref.shape[1]
     pairs = run.shape[0] - 1
-    wide = r_v.shape[4]
-    thin = wide // 2
     rest = n_blk // 2
-    piece, straight = shares(half_rows, chips)
-
-    def at_chip(e):
-        return lax.rem(z + e, chips)
+    sizes, starts = shares(half_rows, chips)
+    plain_start = sum(sizes)
+    straight = half_rows - plain_start
+
+    def facing(n):
+        return across(z, chips - 1 - n, chips)
 
     mine = pl.ds(pl.multiple_of(core * half_rows, half_rows), half_rows)
     get_psi = pltpu.make_async_copy(psi_hbm.at[mine], psi_v.at[0], s_load.at[0])
     get_left = pltpu.make_async_copy(left_hbm, left_in, s_load.at[1])
 
-    def get_r(j):
-        return pltpu.make_async_copy(
-            r_hbm.at[:, :, pl.ds(j * wide, wide)], r_v.at[0, j], s_r.at[j]
-        )
+    def get_r(r):
+        return pltpu.make_async_copy(r_hbm.at[r], r_v.at[0, r], s_r.at[r])
 
     get_psi.start()
-    get_left.start()
-    for j in range(chips):
-        get_r(j).start()
-
-    greet(
-        [partner]
-        + [(z * 2 + k, peers[d]) for d in order for k in range(2)]
-        + [(at_chip(e) * 2 + core, c) for e in range(1, chips)]
-    )
+
+    def by_chip(run_one):
+        for chip in range(chips):
+            @pl.when(z == chip)
+            def _(chip=chip):
+                run_one(chip)
+
+    barrier = pltpu.get_barrier_semaphore()
+    plane = [partner] + [(z * 2 + k, peers[d]) for d in order for k in range(2)]
+    for to in plane:
+        pl.semaphore_signal(barrier, inc=1, device_id=to, device_id_type=MESH)
+    for e in range(1, chips):
+        @pl.when(z + e < chips)
+        def _(e=e):
+            to = (g + 2 * e, c)
+            pl.semaphore_signal(barrier, inc=1, device_id=to, device_id_type=MESH)
+    with scope("greet"):
+        by_chip(lambda chip: pl.semaphore_wait(barrier, len(plane) + chip))
+    for e in range(1, chips):
+        @pl.when(z >= e)
+        def _(e=e):
+            to = (g - 2 * e, c)
+            pl.semaphore_signal(above.at[z], inc=1, device_id=to, device_id_type=MESH)
 
     def rows_of(chip):
-        return pl.ds(pl.multiple_of(chip * piece, piece), piece)
-
-    rest_rows = pl.ds(piece * chips, straight)
-
-    def first(d):
-        return remote(
-            psi_v.at[0, rows_of(z)], psi_v.at[d, rows_of(z)], ss_a.at[d], sr_a.at[d], (g, peers[d])
+        return pl.ds(starts[chip], sizes[chip])
+
+    rest_rows = pl.ds(plain_start, straight)
+
+    near_d = [1] + list(range(2, n_blk, 2))
+    far_d = list(range(3, n_blk, 2))
+
+    def first(d, chip):
+        rows = rows_of(chip)
+        return remote(
+            psi_v.at[0, rows], psi_v.at[d, rows], ss_a.at[d], sr_a.at[d], (g, peers[d])
         )
 
     def plain(d):
@@ -105,32 +116,44 @@
             psi_v.at[0, rest_rows], psi_v.at[d, rest_rows], ss_c.at[d], sr_c.at[d], (g, peers[d])
         )
 
-    def along(d, e):
-        here = psi_v.at[d, rows_of(z)]
-        return remote(here, here, ss_z.at[d, e], sr_z.at[d, z], (at_chip(e) * 2 + core, c))
-
-    def passed(d, way):
-        source, to = (0, chips - 1) if way == 0 else (chips - 1, 0)
+    def second(d, way, chip):
+        source, to = (d - 1, 1) if way == 0 else (1, d - 1)
+        at = pl.ds(starts[chip] + way * (sizes[chip] // 2), sizes[chip] // 2)
+        return remote(
+            psi_v.at[source, at], psi_v.at[d, at], ss_f.at[d, way], sr_f.at[d, way], (g, peers[to])
+        )
+
+    def plain_second(d, way):
+        source, to = (d - 1, 1) if way == 0 else (1, d - 1)
+        at = pl.ds(plain_start + way * (straight // 2), straight // 2)
+        return remote(
+            psi_v.at[source, at], psi_v.at[d, at], ss_g.at[d, way], sr_g.at[d, way], (g, peers[to])
+        )
+
+    def along(d, chip, to):
+        here = psi_v.at[d, rows_of(chip)]
+        return remote(here, here, ss_z.at[d, to], sr_z.at[d, chip], (to * 2 + core, c))
+
+    def passed(d, source, to):
         here = psi_v.at[d, rows_of(source)]
-        return remote(here, here, ss_y.at[d, way], sr_z.at[d, source], (to * 2 + core, c))
+        return remote(here, here, ss_y.at[d, source], sr_z.at[d, source], (to * 2 + core, c))
 
     def arrived(d, source):
         here = psi_v.at[d, rows_of(source)]
         return remote(here, here, ss_z.at[d, 0], sr_z.at[d, source], partner)
 
-    relay = chips > 2
-
-    def near(e):
-        if not relay:
-            return True
-        to = at_chip(e)
-        return jnp.logical_and(to - z < chips - 1, z - to < chips - 1)
-
-    def relays(way):
-        return z == (chips - 2 if way == 0 else 1)
-
-    def swap_r(j):
-        return remote(r_v.at[0, j], r_v.at[1, j], ss_r.at[j], sr_r.at[j], partner)
+    relays = []
+    if chips > 2:
+        relays.append((chips - 2, list(range(chips - 3, -1, -1)), chips - 1))
+        relays.append((1, list(range(2, chips)), 0))
+
+    def targets(chip):
+        skip = [to for _, sources, to in relays if chip in sources]
+        found = [to for to in range(chips) if to != chip and to not in skip]
+        return sorted(found, key=lambda to: -abs(to - chip))
+
+    def swap_r(r):
+        return remote(r_v.at[0, r], r_v.at[1, r], ss_r.at[r], sr_r.at[r], partner)
 
     def lefts(d, k):
         which = core if k == 0 else 1 - core
@@ -143,19 +166,28 @@
 
     table = remote(tab_v.at[0], tab_v.at[1], ss_t, sr_t, partner)
 
-    get_psi.wait()
-    for d in order:
-        first(d).start()
-    for d in order:
-        if straight:
-            plain(d).start()
+    def start_plane(chip):
+        for d in near_d:
+            first(d, chip).start()
+
+    with scope("psi"):
+        get_psi.wait()
+        get_left.start()
+    with scope("start_plane"):
+        by_chip(start_plane)
+        for d in near_d:
+            if straight:
+                plain(d).start()
+    for r in range(local_ops):
+        get_r(r).start()
 
     tab_v[0] = jnp.zeros_like(tab_v[0])
     for j in range(group):
         tab_v[0, j : j + 1, :blocks] = target_ref[pl.ds(lax.rem(pair_ref[j], group), 1), :]
     table.start()
 
-    get_left.wait()
+    with scope("left"):
+        get_left.wait()
     lane = lax.broadcasted_iota(jnp.int32, (1, block_rows), 1)
 
     def put(j, carry):
@@ -169,33 +201,43 @@
         return carry
 
     lax.fori_loop(0, group, put, 0)
-    for d in order:
+    def spread_near(chip):
+        first(1, chip).wait_recv()
+        for f in far_d:
+            second(f, 1, chip).start()
+        for d in near_d[1:]:
+            first(d, chip).wait_recv()
+            second(d + 1, 0, chip).start()
+        for to in range(chip + 1, chips):
+            pl.semaphore_wait(above.at[to], 1)
+        for d in near_d:
+            for to in targets(chip):
+                along(d, chip, to).start()
+
+    with scope("spread_near"):
+        by_chip(spread_near)
+    for d in near_d:
         for k in range(2):
             lefts(d, k).start()
-    for j in range(chips):
-        get_r(j).wait()
-        swap_r(j).start()
+    for r in range(local_ops):
+        get_r(r).wait()
+        swap_r(r).start()
     lefts(0, 1).start()
     left_v[0, 0] = stage[core, pl.ds(c * local_ops, local_ops)]
     run[pairs] = jnp.zeros_like(run[pairs])
 
     def image(d, k):
-        def one(j, carry):
-            for r in range(local_ops):
-                out = jnp.dot(psi_v[d], r_v[k, j, r], preferred_element_type=F32)
-                img[j, d, k, r] = out.astype(BF16).reshape(half_blocks, block_rows, wide)
+        def one(r, carry):
+            out = jnp.dot(psi_v[d], r_v[k, r], preferred_element_type=F32).astype(BF16)
+            for j in range(chips):
+                piece = out[:, j * wide : (j + 1) * wide]
+                img[j, d, k, r] = piece.reshape(half_blocks, block_rows, wide)
             return carry
 
-        lax.fori_loop(0, chips, one, 0)
-
-    image(0, 0)
-    for d in order:
-        first(d).wait_recv()
-        for e in others:
-            @pl.when(near(e))
-            def _(d=d, e=e):
-                along(d, e).start()
-
+        lax.fori_loop(0, local_ops, one, 0)
+
+    with scope("image00"):
+        image(0, 0)
     table.wait_recv()
     get_table = pltpu.make_async_copy(tab_v, tab_s, s_load.at[2])
     get_table.start()
@@ -214,50 +256,73 @@
         prev_s[p] = before
         return tuple(jnp.where(t == b, p, last[b]) for b in range(blocks))
 
-    last = lax.fori_loop(0, pairs, link, (jnp.int32(pairs),) * blocks)
+    with scope("link"):
+        last = lax.fori_loop(0, pairs, link, (jnp.int32(pairs),) * blocks)
     for b in range(blocks):
         last_s[b] = last[b]
 
+    with scope("plain_near"):
+        for d in near_d:
+            if straight:
+                plain(d).wait_recv()
+            for f in far_d:
+                if straight and (d == 1 or d == f - 1):
+                    plain_second(f, 1 if d == 1 else 0).start()
+    for d in far_d:
+        for k in range(2):
+            lefts(d, k).start()
+
+    def spread_far(chip):
+        for d in far_d:
+            for way in range(2):
+                second(d, way, chip).wait_recv()
+            for to in targets(chip):
+                along(d, chip, to).start()
+
+    with scope("spread_far"):
+        by_chip(spread_far)
+
     def pass_on(d):
-        for way in range(2 if relay else 0):
-            @pl.when(relays(way))
-            def _(way=way):
-                arrived(d, 0 if way == 0 else chips - 1).wait_recv()
-                passed(d, way).start()
+        for node, sources, to in relays:
+            @pl.when(z == node)
+            def _(sources=sources, to=to):
+                for source in sources:
+                    arrived(d, source).wait_recv()
+                    passed(d, source, to).start()
 
     def settle(d):
-        for e in range(1, chips):
-            source = at_chip(e)
-            done = False
-            if relay:
-                done = jnp.logical_or(
-                    jnp.logical_and(relays(0), source == 0),
-                    jnp.logical_and(relays(1), source == chips - 1),
-                )
-
-            @pl.when(jnp.logical_not(done))
+        for source in range(chips):
+            due = z != source
+            for node, sources, _ in relays:
+                if source in sources:
+                    due = jnp.logical_and(due, z != node)
+
+            @pl.when(due)
             def _(source=source):
                 arrived(d, source).wait_recv()
-        if straight:
-            plain(d).wait_recv()
-
-    pass_on(1)
-    for j in range(chips):
-        swap_r(j).wait_recv()
-    image(0, 1)
+        if straight and d in far_d:
+            for way in range(2):
+                plain_second(d, way).wait_recv()
+
+    with scope("pass#d=1"):
+        pass_on(1)
+    with scope("swapr"):
+        for r in range(local_ops):
+            swap_r(r).wait_recv()
+    with scope("image01"):
+        image(0, 1)
     for d in order:
         if d + 1 < n_blk:
-            pass_on(d + 1)
-        settle(d)
-        for k in range(2):
-            image(d, k)
-    lefts(0, 1).wait_recv()
-    for d in order:
-        for k in range(2):
-            lefts(d, k).wait_recv()
+            with scope("pass#d=%d" % (d + 1)):
+                pass_on(d + 1)
+        with scope("settle#d=%d" % d):
+            settle(d)
+        with scope("image#d=%d" % d):
+            image(d, 0)
+            image(d, 1)
 
     def mix(n):
-        j = at_chip(n + 1)
+        j = facing(n)
 
         def one(p, carry):
             i = p % half_blocks
@@ -268,7 +333,15 @@
             run[p] = run[prev_s[p]] + mixed
             return carry
 
-        lax.fori_loop(0, pairs, one, 0, unroll=4)
+        if n == 0:
+            each = pairs // n_blk
+            lefts(0, 1).wait_recv()
+            for d in range(n_blk):
+                for k in range(2 if d else 0):
+                    lefts(d, k).wait_recv()
+                lax.fori_loop(d * each, (d + 1) * each, one, 0, unroll=min(each, 8))
+        else:
+            lax.fori_loop(0, pairs, one, 0, unroll=8)
 
         def emit(d, carry):
             for i in range(local_blocks):
@@ -307,7 +380,7 @@
 
     def last_step(n):
         return remote(
-            send3.at[n], recv3.at[n], ss_3.at[n], sr_3.at[n], (at_chip(n + 1) * 2 + core, c)
+            send3.at[n], recv3.at[n], ss_3.at[n], sr_3.at[n], (facing(n) * 2 + core, c)
         )
 
     def join(n):
@@ -363,34 +436,52 @@
             kept = jnp.where(row < len_ref[c * local_blocks + i], kept, jnp.zeros_like(kept))
             out_ref[i * block_rows : (i + 1) * block_rows] = kept.astype(out_ref.dtype)
 
-    for n in range(chips + 3):
-        if n < chips:
-            mix(n)
-        if 0 <= n - 1 < chips:
-            join(n - 1)
-        if 0 <= n - 2 < chips:
-            middle(n - 2)
-        if 0 <= n - 3 < chips:
-            finish(n - 3)
+    def perform(stage_of, n):
+        with scope("%s#n=%d" % (stage_of.__name__, n)):
+            stage_of(n)
+
+    perform(mix, 0)
+    for n in range(1, chips):
+        perform(mix, n)
+        if n < 3:
+            perform(join, n - 1)
+    for n in range(chips):
+        perform(middle, n)
+        if n:
+            perform(finish, n - 1)
+        if 2 <= n + 2 < chips:
+            perform(join, n + 2)
+    perform(finish, chips - 1)
 
     table.wait_send()
     lefts(0, 1).wait_send()
-    for j in range(chips):
-        swap_r(j).wait_send()
+    for r in range(local_ops):
+        swap_r(r).wait_send()
+
+    def drain(chip):
+        for d in near_d:
+            first(d, chip).wait_send()
+        for d in far_d:
+            for way in range(2):
+                second(d, way, chip).wait_send()
+        for d in order:
+            for to in targets(chip):
+                along(d, chip, to).wait_send()
+
+    by_chip(drain)
     for d in order:
-        first(d).wait_send()
-        if straight:
-            plain(d).wait_send()
+        for node, sources, to in relays:
+            @pl.when(z == node)
+            def _(d=d, sources=sources, to=to):
+                for source in sources:
+                    passed(d, source, to).wait_send()
         for k in range(2):
             lefts(d, k).wait_send()
-        for e in others:
-            @pl.when(near(e))
-            def _(d=d, e=e):
-                along(d, e).wait_send()
-        for way in range(2 if relay else 0):
-            @pl.when(relays(way))
-            def _(d=d, way=way):
-                passed(d, way).wait_send()
+    for d in near_d if straight else []:
+        plain(d).wait_send()
+    for d in far_d if straight else []:
+        for way in range(2):
+            plain_second(d, way).wait_send()
     for n in range(chips):
         swap(n).wait_send()
         step_a1(n).wait_send()
@@ -422,7 +513,7 @@
 
     return pl.pallas_call(
         functools.partial(sigma_kernel, n_ops, n_blk),
-        out_shape=jax.ShapeDtypeStruct((my_rows, thin), BF16),
+        out_shape=pltpu.VMEM((my_rows, thin), BF16),
         in_specs=[in_hbm, in_hbm, in_hbm, in_vmem, in_smem, in_smem],
         out_specs=in_vmem,
         scratch_shapes=[
@@ -430,7 +521,7 @@
             VMEM(left_blocks.shape, BF16),
             VMEM((2, group, half_blocks, block_rows, block_rows), BF16),
             VMEM((n_blk, 2, local_ops, half_blocks, block_rows, block_rows), BF16),
-            VMEM((2, chips, local_ops, columns, wide), BF16),
+            VMEM((2, local_ops, columns, columns), BF16),
             VMEM((chips, n_blk, 2, local_ops, half_blocks, block_rows, wide), BF16),
             VMEM((pairs + 1, block_rows, wide), F32),
             VMEM((2, group, 128), jnp.int32),
@@ -448,10 +539,10 @@
             VMEM((chips, half_rows, thin), BF16),
             VMEM((chips, 2, half_rows, thin), BF16),
             VMEM((chips, 2, half_rows, thin), BF16),
-            DMA((3,)), DMA((chips,)),
-            *dmas((n_blk,), (n_blk,), (n_blk, 2), (n_blk, chips)),
-            DMA((n_blk, 2)),
-            *dmas((chips,), ()),
+            DMA((3,)), DMA((local_ops,)),
+            *dmas((n_blk,), (n_blk,), (n_blk, 2), (n_blk, 2), (n_blk, 2), (n_blk, chips)),
+            DMA((n_blk, chips)), pltpu.SemaphoreType.REGULAR((chips,)),
+            *dmas((local_ops,), ()),
             *dmas((chips,), (chips,), (chips, rest), (chips, rest), (chips,), (chips,)),
         ],
         compiler_params=pltpu.CompilerParams(

time: 65.4 us -> 56.9 us (0.87)
  Pallas kernels: 63.6 us -> 56 us
  local copies, waits for them, and re-layouts: 1.57 us -> 0.66 us
    pallas_call x1, Pallas kernels: 63.6 us -> 56 us  [local(): pl.pallas_call(functools.partial(sigma_kernel, n_ops, n_blk), out_shape=p...]
    unnamed x1, local copies, waits for them, and re-layouts: 1.57 us -> 0.66 us
where the time goes in v2:
time: 56.9 us; the launch traced here: 56.7 us
  Pallas kernels  56 us (98%)
  local copies, waits for them, and re-layouts  0.66 us (1%)
    pallas_call x1, Pallas kernels, local(): pl.pallas_call(functools.partial(sigma_kernel, n_ops, n_blk), out_shape=p...  56 us

profile of v2, /device:TPU:0, one launch (start us, length us, event | category | flops | bytes accessed | tf_op | source)
XLA Modules:
  0.0 56.7 jit_solution(12957351057811530971)
XLA Ops:
  0.0 56.0 %sigma.1 = bf16[512,128]{1,0:T(8,128)(2,1)S(1)} custom-call(bf16[512,1024]{1,0:T(8,128)(2,1)} %psi_hbm.1, bf16[8,4,128,128]{3,2,1,0:T(8,128)(2,1)} %left_hbm.1, bf16[2,1024,1024]{2,1,0:T(8,128)(2,1)} %r_hbm.1, s32[8,16]{1,0:T(8,128)} %target_ref.1, s32[8]{0:T(128)} %pair_ref.1, s32[16]{0:T(128)} %len_ref.1), custom_call_target="tpu_custom_call" | custom-call | tf_op jit(solution)/shard_map/sigma/pallas_call | solution.py:514
  56.0 0.7 %copy.8 = bf16[512,128]{1,0:T(8,128)(2,1)} copy(bf16[512,128]{1,0:T(8,128)(2,1)S(1)} %sigma.1) | data formatting | bytes 262144

commit v3 on v2

--- a/solution.py
+++ b/solution.py
@@ -37,10 +37,10 @@
 
 def sigma_kernel(
     n_ops, n_blk, psi_hbm, left_hbm, r_hbm, target_ref, pair_ref, len_ref, out_ref,
-    psi_v, left_in, stage, left_v, r_v, img, run, tab_v, tab_s, prev_s, last_s,
-    part, recv1, sum1, recv_a1, recv_b1, send_a2, recv_a2, send_b2, recv_b2, send3, recv3,
+    own, psi_z, psi_p, left_in, stage, left_v, r_v, img, run, tab_v, tab_s, prev_s, last_s,
+    part, recv1, sum1, recv_z, recv_a1, recv_b1, send_a2, recv_a2, send_b2, recv_b2, send3, recv3,
     s_load, s_r, ss_a, sr_a, ss_c, sr_c, ss_f, sr_f, ss_g, sr_g, ss_l, sr_l, ss_z, sr_z, ss_y, above, ss_r, sr_r, ss_t, sr_t,
-    ss_1, sr_1, ss_a1, sr_a1, ss_b1, sr_b1, ss_a2, sr_a2, ss_b2, sr_b2, ss_3, sr_3,
+    ss_1, sr_1, ss_f1, sr_f1, ss_a1, sr_a1, ss_b1, sr_b1, ss_a2, sr_a2, ss_b2, sr_b2, ss_3, sr_3,
 ):
     g, c = lax.axis_index("ops"), lax.axis_index("blk")
     chips = n_ops // 2
@@ -49,7 +49,8 @@
     peers = [across(c, d, n_blk) for d in range(n_blk)]
     order = list(range(1, n_blk))
 
-    half_rows, columns = psi_v.shape[1:]
+    columns = psi_hbm.shape[1]
+    half_rows = psi_hbm.shape[0] // 2
     group, local_blocks, block_rows, _ = left_in.shape
     half_blocks = local_blocks // 2
     local_ops = r_hbm.shape[0]
@@ -59,14 +60,15 @@
     pairs = run.shape[0] - 1
     rest = n_blk // 2
     sizes, starts = shares(half_rows, chips)
-    plain_start = sum(sizes)
-    straight = half_rows - plain_start
+    climb = sum(sizes)
+    straight = half_rows - climb
+    ahead = recv_z.shape[3]
 
     def facing(n):
         return across(z, chips - 1 - n, chips)
 
     mine = pl.ds(pl.multiple_of(core * half_rows, half_rows), half_rows)
-    get_psi = pltpu.make_async_copy(psi_hbm.at[mine], psi_v.at[0], s_load.at[0])
+    get_psi = pltpu.make_async_copy(psi_hbm.at[mine], own, s_load.at[0])
     get_left = pltpu.make_async_copy(left_hbm, left_in, s_load.at[1])
 
     def get_r(r):
@@ -100,52 +102,50 @@
     def rows_of(chip):
         return pl.ds(starts[chip], sizes[chip])
 
-    rest_rows = pl.ds(plain_start, straight)
-
     near_d = [1] + list(range(2, n_blk, 2))
     far_d = list(range(3, n_blk, 2))
 
     def first(d, chip):
         rows = rows_of(chip)
         return remote(
-            psi_v.at[0, rows], psi_v.at[d, rows], ss_a.at[d], sr_a.at[d], (g, peers[d])
+            own.at[rows], psi_z.at[d, rows], ss_a.at[d], sr_a.at[d], (g, peers[d])
         )
 
     def plain(d):
         return remote(
-            psi_v.at[0, rest_rows], psi_v.at[d, rest_rows], ss_c.at[d], sr_c.at[d], (g, peers[d])
+            own.at[pl.ds(climb, straight)], psi_p.at[d], ss_c.at[d], sr_c.at[d], (g, peers[d])
         )
 
     def second(d, way, chip):
         source, to = (d - 1, 1) if way == 0 else (1, d - 1)
         at = pl.ds(starts[chip] + way * (sizes[chip] // 2), sizes[chip] // 2)
         return remote(
-            psi_v.at[source, at], psi_v.at[d, at], ss_f.at[d, way], sr_f.at[d, way], (g, peers[to])
+            psi_z.at[source, at], psi_z.at[d, at], ss_f.at[d, way], sr_f.at[d, way], (g, peers[to])
         )
 
     def plain_second(d, way):
         source, to = (d - 1, 1) if way == 0 else (1, d - 1)
-        at = pl.ds(plain_start + way * (straight // 2), straight // 2)
-        return remote(
-            psi_v.at[source, at], psi_v.at[d, at], ss_g.at[d, way], sr_g.at[d, way], (g, peers[to])
+        at = pl.ds(way * (straight // 2), straight // 2)
+        return remote(
+            psi_p.at[source, at], psi_p.at[d, at], ss_g.at[d, way], sr_g.at[d, way], (g, peers[to])
         )
 
     def along(d, chip, to):
-        here = psi_v.at[d, rows_of(chip)]
+        here = psi_z.at[d, rows_of(chip)]
         return remote(here, here, ss_z.at[d, to], sr_z.at[d, chip], (to * 2 + core, c))
 
     def passed(d, source, to):
-        here = psi_v.at[d, rows_of(source)]
+        here = psi_z.at[d, rows_of(source)]
         return remote(here, here, ss_y.at[d, source], sr_z.at[d, source], (to * 2 + core, c))
 
     def arrived(d, source):
-        here = psi_v.at[d, rows_of(source)]
+        here = psi_z.at[d, rows_of(source)]
         return remote(here, here, ss_z.at[d, 0], sr_z.at[d, source], partner)
 
     relays = []
     if chips > 2:
-        relays.append((chips - 2, list(range(chips - 3, -1, -1)), chips - 1))
-        relays.append((1, list(range(2, chips)), 0))
+        relays.append((chips - 2, [0], chips - 1))
+        relays.append((1, [chips - 1], 0))
 
     def targets(chip):
         skip = [to for _, sources, to in relays if chip in sources]
@@ -217,8 +217,7 @@
     with scope("spread_near"):
         by_chip(spread_near)
     for d in near_d:
-        for k in range(2):
-            lefts(d, k).start()
+        lefts(d, 0).start()
     for r in range(local_ops):
         get_r(r).wait()
         swap_r(r).start()
@@ -226,18 +225,30 @@
     left_v[0, 0] = stage[core, pl.ds(c * local_ops, local_ops)]
     run[pairs] = jnp.zeros_like(run[pairs])
 
-    def image(d, k):
+    def image(state, first_d, count, at, k):
+        rows = state.shape[0] // count
+
         def one(r, carry):
-            out = jnp.dot(psi_v[d], r_v[k, r], preferred_element_type=F32).astype(BF16)
-            for j in range(chips):
-                piece = out[:, j * wide : (j + 1) * wide]
-                img[j, d, k, r] = piece.reshape(half_blocks, block_rows, wide)
+            out = jnp.dot(state[...], r_v[k, r], preferred_element_type=F32).astype(BF16)
+            for d in range(count):
+                for j in range(chips):
+                    img[j, first_d + d, k, r, at : at + rows] = out[
+                        d * rows : (d + 1) * rows, j * wide : (j + 1) * wide
+                    ]
             return carry
 
         lax.fori_loop(0, local_ops, one, 0)
 
+    def image_z(first_d, count, k):
+        image(psi_z[first_d : first_d + count].reshape(count * climb, columns), first_d, count, 0, k)
+
+    def image_p(first_d, count, k):
+        if straight:
+            state = psi_p[first_d : first_d + count].reshape(count * straight, columns)
+            image(state, first_d, count, climb, k)
+
     with scope("image00"):
-        image(0, 0)
+        image(own, 0, 1, 0, 0)
     table.wait_recv()
     get_table = pltpu.make_async_copy(tab_v, tab_s, s_load.at[2])
     get_table.start()
@@ -268,6 +279,8 @@
             for f in far_d:
                 if straight and (d == 1 or d == f - 1):
                     plain_second(f, 1 if d == 1 else 0).start()
+    for d in near_d:
+        lefts(d, 1).start()
     for d in far_d:
         for k in range(2):
             lefts(d, k).start()
@@ -300,26 +313,36 @@
             @pl.when(due)
             def _(source=source):
                 arrived(d, source).wait_recv()
-        if straight and d in far_d:
-            for way in range(2):
-                plain_second(d, way).wait_recv()
-
     with scope("pass#d=1"):
         pass_on(1)
     with scope("swapr"):
         for r in range(local_ops):
             swap_r(r).wait_recv()
     with scope("image01"):
-        image(0, 1)
-    for d in order:
-        if d + 1 < n_blk:
-            with scope("pass#d=%d" % (d + 1)):
-                pass_on(d + 1)
+        image(own, 0, 1, 0, 1)
+    tail_d = far_d[-1]
+    for d in order[1:]:
+        with scope("pass#d=%d" % d):
+            pass_on(d)
+        if d < tail_d and d % 2 == 0:
+            with scope("image_p#d=%d" % d):
+                for k in range(2):
+                    image_p(d - 1, 2, k)
+    with scope("plain_far"):
+        for d in far_d if straight else []:
+            for way in range(2):
+                plain_second(d, way).wait_recv()
+    with scope("image_p_far"):
+        for k in range(2):
+            image_p(tail_d, 1, k)
+    for d in range(1, n_blk, 2):
+        count = min(2, n_blk - d)
         with scope("settle#d=%d" % d):
-            settle(d)
-        with scope("image#d=%d" % d):
-            image(d, 0)
-            image(d, 1)
+            for e in range(count):
+                settle(d + e)
+        with scope("image_z#d=%d" % d):
+            for k in range(2):
+                image_z(d, count, k)
 
     def mix(n):
         j = facing(n)
@@ -329,7 +352,8 @@
             r = p // half_blocks % local_ops
             k = p // (half_blocks * local_ops) % 2
             d = p // (half_blocks * local_ops * 2)
-            mixed = jnp.dot(left_v[d, k, r, i], img[j, d, k, r, i], preferred_element_type=F32)
+            rows = pl.ds(pl.multiple_of(i * block_rows, block_rows), block_rows)
+            mixed = jnp.dot(left_v[d, k, r, i], img[j, d, k, r, rows], preferred_element_type=F32)
             run[p] = run[prev_s[p]] + mixed
             return carry
 
@@ -359,82 +383,141 @@
     def swap(n):
         return remote(part.at[n, 1 - core], recv1.at[n], ss_1.at[n], sr_1.at[n], partner)
 
+    early = pl.ds(0, ahead)
+    late = pl.ds(ahead, half_rows - ahead)
+
+    def moved(n):
+        return early if n == chips else late
+
+    def chunk(n):
+        return min(n, chips - 1)
+
+    def gathers(n):
+        offset = chips - 1 - n
+        return offset > 1 and offset % 2 == 1
+
+    def step_z(n):
+        return remote(
+            sum1.at[n, :, :, early], recv_z.at[n], ss_f1.at[n], sr_f1.at[n], (facing(n) * 2 + core, c)
+        )
+
     def step_a1(n):
         return remote(
-            sum1.at[n, 0, pl.ds(rest, rest)], recv_a1.at[n], ss_a1.at[n], sr_a1.at[n], (g, peers[1])
+            sum1.at[chunk(n), 0, pl.ds(rest, rest), moved(n)], recv_a1.at[chunk(n), :, moved(n)],
+            ss_a1.at[n], sr_a1.at[n], (g, peers[1]),
         )
 
     def step_b1(n, dy):
         return remote(
-            sum1.at[n, 1, pl.ds(2 * dy, 2)], recv_b1.at[n, dy],
+            sum1.at[chunk(n), 1, pl.ds(2 * dy, 2), moved(n)], recv_b1.at[chunk(n), dy, :, moved(n)],
             ss_b1.at[n, dy], sr_b1.at[n, dy], (g, peers[2 * dy]),
         )
 
     def step_a2(n, dy):
         return remote(
-            send_a2.at[n, dy], recv_a2.at[n, dy], ss_a2.at[n, dy], sr_a2.at[n, dy], (g, peers[2 * dy])
+            send_a2.at[chunk(n), dy, moved(n)], recv_a2.at[chunk(n), dy, moved(n)],
+            ss_a2.at[n, dy], sr_a2.at[n, dy], (g, peers[2 * dy]),
         )
 
     def step_b2(n):
-        return remote(send_b2.at[n], recv_b2.at[n], ss_b2.at[n], sr_b2.at[n], (g, peers[1]))
+        return remote(
+            send_b2.at[chunk(n), moved(n)], recv_b2.at[chunk(n), moved(n)],
+            ss_b2.at[n], sr_b2.at[n], (g, peers[1]),
+        )
 
     def last_step(n):
         return remote(
-            send3.at[n], recv3.at[n], ss_3.at[n], sr_3.at[n], (facing(n) * 2 + core, c)
-        )
+            send3.at[n, :, moved(n)], recv3.at[n, :, moved(n)],
+            ss_3.at[n], sr_3.at[n], (facing(chips - 2 if gathers(n) else n) * 2 + core, c),
+        )
+
+    def add(n, half, slots):
+        m, rows = chunk(n), moved(n)
+        both = part[m, core, half, slots, rows].astype(F32) + recv1[m, half, slots, rows].astype(F32)
+        if n == chips:
+            for e in range(chips - 1):
+                both += recv_z[e, half, slots].astype(F32)
+        sum1[m, half, slots, rows] = both.astype(BF16)
+
+    def begin(n):
+        if n == 0:
+            join(n)
+        else:
+            swap(n).wait_recv()
+        for half in range(2):
+            both = part[n, core, half, :, early].astype(F32) + recv1[n, half, :, early].astype(F32)
+            sum1[n, half, :, early] = both.astype(BF16)
+        step_z(n).start()
 
     def join(n):
-        swap(n).wait_recv()
-
-        def add(half, slots):
-            both = part[n, core, half, slots].astype(F32) + recv1[n, half, slots].astype(F32)
-            sum1[n, half, slots] = both.astype(BF16)
-
-        add(0, pl.ds(rest, rest))
+        if n in (0, chips - 1):
+            swap(n).wait_recv()
+        if n == chips:
+            for e in range(chips - 1):
+                step_z(e).wait_recv()
+        add(n, 0, pl.ds(rest, rest))
         step_a1(n).start()
-        add(1, pl.ds(2, n_blk - 2))
+        add(n, 1, pl.ds(2, n_blk - 2))
         for dy in range(1, rest):
             step_b1(n, dy).start()
-        add(0, pl.ds(0, rest))
-        add(1, pl.ds(0, 2))
+        add(n, 0, pl.ds(0, rest))
+        add(n, 1, pl.ds(0, 2))
 
     def middle(n):
+        m, rows = chunk(n), moved(n)
         step_a1(n).wait_recv()
         for dy in range(1, rest):
-            both = sum1[n, 0, dy].astype(F32) + recv_a1[n, dy].astype(F32)
-            send_a2[n, dy] = both.astype(BF16)
+            both = sum1[m, 0, dy, rows].astype(F32) + recv_a1[m, dy, rows].astype(F32)
+            send_a2[m, dy, rows] = both.astype(BF16)
             step_a2(n, dy).start()
-        both = sum1[n, 1, 1].astype(F32)
+        both = sum1[m, 1, 1, rows].astype(F32)
         for dy in range(1, rest):
             step_b1(n, dy).wait_recv()
-            both += recv_b1[n, dy, 1].astype(F32)
-        send_b2[n] = both.astype(BF16)
+            both += recv_b1[m, dy, 1, rows].astype(F32)
+        send_b2[m, rows] = both.astype(BF16)
         step_b2(n).start()
 
+    row = lax.broadcasted_iota(jnp.int32, (block_rows, 1), 0)
+
+    def put_out(half, value, first_row):
+        size = value.shape[0]
+        for i in range(half_blocks):
+            low = max(first_row, i * block_rows)
+            high = min(first_row + size, (i + 1) * block_rows)
+            if low < high:
+                kept = value[low - first_row : high - first_row]
+                live = row[low - i * block_rows : high - i * block_rows] < len_ref[
+                    c * local_blocks + half * half_blocks + i
+                ]
+                kept = jnp.where(live, kept, jnp.zeros_like(kept)).astype(out_ref.dtype)
+                out_ref[half * half_rows + low : half * half_rows + high] = kept
+
     def finish(n):
-        a = sum1[n, 0, 0].astype(F32) + recv_a1[n, 0].astype(F32)
-        b = sum1[n, 1, 0].astype(F32)
+        m, rows = chunk(n), moved(n)
+        a = sum1[m, 0, 0, rows].astype(F32) + recv_a1[m, 0, rows].astype(F32)
+        b = sum1[m, 1, 0, rows].astype(F32)
         for dy in range(1, rest):
             step_a2(n, dy).wait_recv()
-            a += recv_a2[n, dy].astype(F32)
-            b += recv_b1[n, dy, 0].astype(F32)
+            a += recv_a2[m, dy, rows].astype(F32)
+            b += recv_b1[m, dy, 0, rows].astype(F32)
         step_b2(n).wait_recv()
-        b += recv_b2[n].astype(F32)
+        b += recv_b2[m, rows].astype(F32)
+        if 0 < n < chips - 1 and gathers(n - 1):
+            last_step(n - 1).wait_recv()
+            a += recv3[n - 1, 0, rows].astype(F32)
+            b += recv3[n - 1, 1, rows].astype(F32)
         if n < chips - 1:
-            send3[n, 0] = a.astype(BF16)
-            send3[n, 1] = b.astype(BF16)
+            send3[n, 0, rows] = a.astype(BF16)
+            send3[n, 1, rows] = b.astype(BF16)
             last_step(n).start()
             return
-        for e in range(chips - 1):
-            last_step(e).wait_recv()
-            a += recv3[e, 0].astype(F32)
-            b += recv3[e, 1].astype(F32)
-        row = lax.broadcasted_iota(jnp.int32, (block_rows, 1), 0)
-        for i in range(local_blocks):
-            at = i % half_blocks * block_rows
-            kept = (a if i < half_blocks else b)[at : at + block_rows]
-            kept = jnp.where(row < len_ref[c * local_blocks + i], kept, jnp.zeros_like(kept))
-            out_ref[i * block_rows : (i + 1) * block_rows] = kept.astype(out_ref.dtype)
+        if n == chips - 1:
+            for e in [e for e in range(chips - 1) if not gathers(e)]:
+                last_step(e).wait_recv()
+                a += recv3[e, 0, rows].astype(F32)
+                b += recv3[e, 1, rows].astype(F32)
+        put_out(0, a, 0 if n == chips else ahead)
+        put_out(1, b, 0 if n == chips else ahead)
 
     def perform(stage_of, n):
         with scope("%s#n=%d" % (stage_of.__name__, n)):
@@ -443,14 +526,19 @@
     perform(mix, 0)
     for n in range(1, chips):
         perform(mix, n)
-        if n < 3:
-            perform(join, n - 1)
+        perform(begin, n - 1)
+        if n == 2:
+            perform(join, 1)
     for n in range(chips):
         perform(middle, n)
         if n:
             perform(finish, n - 1)
         if 2 <= n + 2 < chips:
             perform(join, n + 2)
+        if n == chips - 2:
+            perform(join, chips)
+    perform(middle, chips)
+    perform(finish, chips)
     perform(finish, chips - 1)
 
     table.wait_send()
@@ -482,15 +570,18 @@
     for d in far_d if straight else []:
         for way in range(2):
             plain_second(d, way).wait_send()
+    for n in range(chips - 1):
+        step_z(n).wait_send()
     for n in range(chips):
         swap(n).wait_send()
+        if n < chips - 1:
+            last_step(n).wait_send()
+    for n in range(chips + 1):
         step_a1(n).wait_send()
         step_b2(n).wait_send()
         for dy in range(1, rest):
             step_b1(n, dy).wait_send()
             step_a2(n, dy).wait_send()
-        if n < chips - 1:
-            last_step(n).wait_send()
 
 
 def local(n_ops, n_blk, psi, left_blocks, right_ops, block_target, left_partner, block_len):
@@ -517,12 +608,14 @@
         in_specs=[in_hbm, in_hbm, in_hbm, in_vmem, in_smem, in_smem],
         out_specs=in_vmem,
         scratch_shapes=[
-            VMEM((n_blk, half_rows, columns), BF16),
+            VMEM((half_rows, columns), BF16),
+            VMEM((n_blk, sum(shares(half_rows, chips)[0]), columns), BF16),
+            VMEM((n_blk, max(half_rows - sum(shares(half_rows, chips)[0]), 16), columns), BF16),
             VMEM(left_blocks.shape, BF16),
             VMEM((2, group, half_blocks, block_rows, block_rows), BF16),
             VMEM((n_blk, 2, local_ops, half_blocks, block_rows, block_rows), BF16),
             VMEM((2, local_ops, columns, columns), BF16),
-            VMEM((chips, n_blk, 2, local_ops, half_blocks, block_rows, wide), BF16),
+            VMEM((chips, n_blk, 2, local_ops, half_rows, wide), BF16),
             VMEM((pairs + 1, block_rows, wide), F32),
             VMEM((2, group, 128), jnp.int32),
             SMEM((2, group, 128), jnp.int32),
@@ -531,6 +624,7 @@
             VMEM((chips, 2, 2, n_blk, half_rows, thin), BF16),
             VMEM((chips, 2, n_blk, half_rows, thin), BF16),
             VMEM((chips, 2, n_blk, half_rows, thin), BF16),
+            VMEM((max(chips - 1, 1), 2, n_blk, max(half_rows * 3 // 16 // 16, 1) * 16, thin), BF16),
             VMEM((chips, rest, half_rows, thin), BF16),
             VMEM((chips, rest, 2, half_rows, thin), BF16),
             VMEM((chips, rest, half_rows, thin), BF16),
@@ -543,7 +637,8 @@
             *dmas((n_blk,), (n_blk,), (n_blk, 2), (n_blk, 2), (n_blk, 2), (n_blk, chips)),
             DMA((n_blk, chips)), pltpu.SemaphoreType.REGULAR((chips,)),
             *dmas((local_ops,), ()),
-            *dmas((chips,), (chips,), (chips, rest), (chips, rest), (chips,), (chips,)),
+            *dmas((chips,), (chips,), (chips + 1,), (chips + 1, rest)),
+            *dmas((chips + 1, rest), (chips + 1,), (chips,)),
         ],
         compiler_params=pltpu.CompilerParams(
             collective_id=0, has_side_effects=True, vmem_limit_bytes=63 * 2**20

time: 56.9 us -> 53.3 us (0.937)
  Pallas kernels: 56 us -> 52.4 us
    pallas_call x1, Pallas kernels: 56 us -> 52.4 us  [local(): pl.pallas_call(functools.partial(sigma_kernel, n_ops, n_blk), out_shape=p...]
where the time goes in v3:
time: 53.3 us; the launch traced here: 53.1 us
  Pallas kernels  52.4 us (98%)
  local copies, waits for them, and re-layouts  0.66 us (1%)
    pallas_call x1, Pallas kernels, local(): pl.pallas_call(functools.partial(sigma_kernel, n_ops, n_blk), out_shape=p...  52.4 us

profile of v3, /device:TPU:0, one launch (start us, length us, event | category | flops | bytes accessed | tf_op | source)
XLA Modules:
  0.0 53.1 jit_solution(16419226700601976272)
XLA Ops:
  0.0 52.4 %sigma.1 = bf16[512,128]{1,0:T(8,128)(2,1)S(1)} custom-call(bf16[512,1024]{1,0:T(8,128)(2,1)} %psi_hbm.1, bf16[8,4,128,128]{3,2,1,0:T(8,128)(2,1)} %left_hbm.1, bf16[2,1024,1024]{2,1,0:T(8,128)(2,1)} %r_hbm.1, s32[8,16]{1,0:T(8,128)} %target_ref.1, s32[8]{0:T(128)} %pair_ref.1, s32[16]{0:T(128)} %len_ref.1), custom_call_target="tpu_custom_call" | custom-call | tf_op jit(solution)/shard_map/sigma/pallas_call | solution.py:605
  52.4 0.7 %copy.8 = bf16[512,128]{1,0:T(8,128)(2,1)} copy(bf16[512,128]{1,0:T(8,128)(2,1)S(1)} %sigma.1) | data formatting | bytes 262144

commit v4 on v3

--- a/solution.py
+++ b/solution.py
@@ -365,7 +365,7 @@
                     lefts(d, k).wait_recv()
                 lax.fori_loop(d * each, (d + 1) * each, one, 0, unroll=min(each, 8))
         else:
-            lax.fori_loop(0, pairs, one, 0, unroll=8)
+            lax.fori_loop(0, pairs, one, 0, unroll=16)
 
         def emit(d, carry):
             for i in range(local_blocks):
@@ -396,10 +396,16 @@
         offset = chips - 1 - n
         return offset > 1 and offset % 2 == 1
 
+    def crosses(n):
+        return 0 < n < chips - 1 and gathers(n - 1)
+
+    final = [n for n in range(chips - 1) if not gathers(n)]
+
+    def toward(n):
+        return (facing(chips - 2 if gathers(n) else n) * 2 + core, c)
+
     def step_z(n):
-        return remote(
-            sum1.at[n, :, :, early], recv_z.at[n], ss_f1.at[n], sr_f1.at[n], (facing(n) * 2 + core, c)
-        )
+        return remote(sum1.at[n, :, :, early], recv_z.at[n], ss_f1.at[n], sr_f1.at[n], toward(n))
 
     def step_a1(n):
         return remote(
@@ -428,14 +434,14 @@
     def last_step(n):
         return remote(
             send3.at[n, :, moved(n)], recv3.at[n, :, moved(n)],
-            ss_3.at[n], sr_3.at[n], (facing(chips - 2 if gathers(n) else n) * 2 + core, c),
+            ss_3.at[n], sr_3.at[n], toward(n),
         )
 
     def add(n, half, slots):
         m, rows = chunk(n), moved(n)
         both = part[m, core, half, slots, rows].astype(F32) + recv1[m, half, slots, rows].astype(F32)
         if n == chips:
-            for e in range(chips - 1):
+            for e in final:
                 both += recv_z[e, half, slots].astype(F32)
         sum1[m, half, slots, rows] = both.astype(BF16)
 
@@ -447,13 +453,21 @@
         for half in range(2):
             both = part[n, core, half, :, early].astype(F32) + recv1[n, half, :, early].astype(F32)
             sum1[n, half, :, early] = both.astype(BF16)
+        if not crosses(n):
+            step_z(n).start()
+
+    def cross(n):
+        step_z(n - 1).wait_recv()
+        for half in range(2):
+            both = sum1[n, half, :, early].astype(F32) + recv_z[n - 1, half].astype(F32)
+            sum1[n, half, :, early] = both.astype(BF16)
         step_z(n).start()
 
     def join(n):
         if n in (0, chips - 1):
             swap(n).wait_recv()
         if n == chips:
-            for e in range(chips - 1):
+            for e in final:
                 step_z(e).wait_recv()
         add(n, 0, pl.ds(rest, rest))
         step_a1(n).start()
@@ -502,7 +516,7 @@
             b += recv_b1[m, dy, 0, rows].astype(F32)
         step_b2(n).wait_recv()
         b += recv_b2[m, rows].astype(F32)
-        if 0 < n < chips - 1 and gathers(n - 1):
+        if crosses(n):
             last_step(n - 1).wait_recv()
             a += recv3[n - 1, 0, rows].astype(F32)
             b += recv3[n - 1, 1, rows].astype(F32)
@@ -512,12 +526,50 @@
             last_step(n).start()
             return
         if n == chips - 1:
-            for e in [e for e in range(chips - 1) if not gathers(e)]:
+            for e in final:
                 last_step(e).wait_recv()
                 a += recv3[e, 0, rows].astype(F32)
                 b += recv3[e, 1, rows].astype(F32)
         put_out(0, a, 0 if n == chips else ahead)
         put_out(1, b, 0 if n == chips else ahead)
+
+    def drain_gather():
+        table.wait_send()
+        lefts(0, 1).wait_send()
+        for r in range(local_ops):
+            swap_r(r).wait_send()
+
+        def drain(chip):
+            for d in near_d:
+                first(d, chip).wait_send()
+            for d in far_d:
+                for way in range(2):
+                    second(d, way, chip).wait_send()
+            for d in order:
+                for to in targets(chip):
+                    along(d, chip, to).wait_send()
+
+        by_chip(drain)
+        for d in order:
+            for node, sources, to in relays:
+                @pl.when(z == node)
+                def _(d=d, sources=sources, to=to):
+                    for source in sources:
+                        passed(d, source, to).wait_send()
+            for k in range(2):
+                lefts(d, k).wait_send()
+        for d in near_d if straight else []:
+            plain(d).wait_send()
+        for d in far_d if straight else []:
+            for way in range(2):
+                plain_second(d, way).wait_send()
+
+    def drain_steps(n):
+        step_a1(n).wait_send()
+        step_b2(n).wait_send()
+        for dy in range(1, rest):
+            step_b1(n, dy).wait_send()
+            step_a2(n, dy).wait_send()
 
     def perform(stage_of, n):
         with scope("%s#n=%d" % (stage_of.__name__, n)):
@@ -530,58 +582,33 @@
         if n == 2:
             perform(join, 1)
     for n in range(chips):
+        if crosses(n):
+            perform(cross, n)
+    for n in range(chips):
+        if n == 1:
+            drain_gather()
         perform(middle, n)
-        if n:
+        if n and n != chips - 2:
             perform(finish, n - 1)
+        if n == chips - 2:
+            perform(finish, n - 1)
+            perform(join, chips)
         if 2 <= n + 2 < chips:
             perform(join, n + 2)
-        if n == chips - 2:
-            perform(join, chips)
+    for n in range(chips):
+        swap(n).wait_send()
+    for n in range(chips - 1):
+        step_z(n).wait_send()
+    for n in range(chips - 2):
+        drain_steps(n)
     perform(middle, chips)
     perform(finish, chips)
     perform(finish, chips - 1)
 
-    table.wait_send()
-    lefts(0, 1).wait_send()
-    for r in range(local_ops):
-        swap_r(r).wait_send()
-
-    def drain(chip):
-        for d in near_d:
-            first(d, chip).wait_send()
-        for d in far_d:
-            for way in range(2):
-                second(d, way, chip).wait_send()
-        for d in order:
-            for to in targets(chip):
-                along(d, chip, to).wait_send()
-
-    by_chip(drain)
-    for d in order:
-        for node, sources, to in relays:
-            @pl.when(z == node)
-            def _(d=d, sources=sources, to=to):
-                for source in sources:
-                    passed(d, source, to).wait_send()
-        for k in range(2):
-            lefts(d, k).wait_send()
-    for d in near_d if straight else []:
-        plain(d).wait_send()
-    for d in far_d if straight else []:
-        for way in range(2):
-            plain_second(d, way).wait_send()
+    for n in range(chips - 2, chips + 1):
+        drain_steps(n)
     for n in range(chips - 1):
-        step_z(n).wait_send()
-    for n in range(chips):
-        swap(n).wait_send()
-        if n < chips - 1:
-            last_step(n).wait_send()
-    for n in range(chips + 1):
-        step_a1(n).wait_send()
-        step_b2(n).wait_send()
-        for dy in range(1, rest):
-            step_b1(n, dy).wait_send()
-            step_a2(n, dy).wait_send()
+        last_step(n).wait_send()
 
 
 def local(n_ops, n_blk, psi, left_blocks, right_ops, block_target, left_partner, block_len):
@@ -624,7 +651,7 @@
             VMEM((chips, 2, 2, n_blk, half_rows, thin), BF16),
             VMEM((chips, 2, n_blk, half_rows, thin), BF16),
             VMEM((chips, 2, n_blk, half_rows, thin), BF16),
-            VMEM((max(chips - 1, 1), 2, n_blk, max(half_rows * 3 // 16 // 16, 1) * 16, thin), BF16),
+            VMEM((max(chips - 1, 1), 2, n_blk, max(half_rows * 7 // 32 // 8, 1) * 8, thin), BF16),
             VMEM((chips, rest, half_rows, thin), BF16),
             VMEM((chips, rest, 2, half_rows, thin), BF16),
             VMEM((chips, rest, half_rows, thin), BF16),

time: 53.3 us -> 52.9 us (level)
  no operation moved by 1% of the time
where the time goes in v4:
time: 52.9 us; the launch traced here: 52.7 us
  Pallas kernels  52.1 us (98%)
  local copies, waits for them, and re-layouts  0.66 us (1%)
    pallas_call x1, Pallas kernels, local(): pl.pallas_call(functools.partial(sigma_kernel, n_ops, n_blk), out_shape=p...  52.1 us

profile of v4, /device:TPU:0, one launch (start us, length us, event | category | flops | bytes accessed | tf_op | source)
XLA Modules:
  0.0 52.7 jit_solution(9221013260930568881)
XLA Ops:
  0.0 52.1 %sigma.1 = bf16[512,128]{1,0:T(8,128)(2,1)S(1)} custom-call(bf16[512,1024]{1,0:T(8,128)(2,1)} %psi_hbm.1, bf16[8,4,128,128]{3,2,1,0:T(8,128)(2,1)} %left_hbm.1, bf16[2,1024,1024]{2,1,0:T(8,128)(2,1)} %r_hbm.1, s32[8,16]{1,0:T(8,128)} %target_ref.1, s32[8]{0:T(128)} %pair_ref.1, s32[16]{0:T(128)} %len_ref.1), custom_call_target="tpu_custom_call" | custom-call | tf_op jit(solution)/shard_map/sigma/pallas_call | solution.py:632
  52.1 0.7 %copy.8 = bf16[512,128]{1,0:T(8,128)(2,1)} copy(bf16[512,128]{1,0:T(8,128)(2,1)S(1)} %sigma.1) | data formatting | bytes 262144
